TPU v7x, 256 devices: a whole 4x4x8 slice. The times are simulated.
256 devices in a mesh: dp: 16 (over x, z_lo), hyper: 16 (over y, z_hi, core).
Axes of the slice: x: 4, y: 4, z: 8 (z_hi: 2, z_lo: 4; z = z_hi * 4 + z_lo), core: 2. Of those that a mesh axis runs over, the one named last changes fastest.
Arguments:
- inputs: bfloat16 [512, 64, 128], P(('dp', 'hyper')), may hold values from -64 to 64
- labels: int32 [512, 64], P(('dp', 'hyper')), may hold values from 0 to 255
- client_ids: int32 [512], P(('dp', 'hyper')), may hold values from 0 to 511
- ext_weight: bfloat16 [128, 4096], replicated, may hold values from -0.5 to 0.5
- ext_bias: bfloat16 [4096], replicated, may hold values from -3 to 3
- embeddings: bfloat16 [512, 128], replicated, may hold values from -1.5 to 1.5
- hyper_in: bfloat16 [128, 50], replicated, may hold values from -2.09375 to 2.09375
- hyper_bias: float32 [50], replicated, may hold values from -3 to 3
- hyper_out: bfloat16 [4096, 50, 256], P('hyper'), may hold values from -0.1796875 to 0.1796875
Outputs:
- grad_ext_weight: float32 [128, 4096], replicated
- grad_ext_bias: float32 [4096], replicated
- grad_embeddings: float32 [512, 128], replicated
- grad_hyper_in: float32 [128, 50], replicated
- grad_hyper_bias: float32 [50], replicated
- grad_hyper_out: float32 [4096, 50, 256], P(('hyper', 'dp'))
Inputs may be any that keep to these rules, and one draw needn't show every extreme that they name: `client_ids`: A client may hold several slots or none.
All inputs are finite; a program needn't handle non-finite values.
Results may differ from a plain program's by a relative error of at most 0.014.
The roundings to bfloat16 on the way count: a program that leaves them out, or rounds other values in their place, can miss the bound.
Values may be sent and summed in bfloat16 or wider, within the bound.
No kernel may reach another device: no remote copies, remote signals or barrier semaphores. Data moves between devices by JAX's collectives and lax.ppermute only.
A program may use at most 128 MiB of HBM per device.

v0:
```python
import jax
import jax.numpy as jnp
from jax import lax
from jax.sharding import Mesh
from jax.sharding import PartitionSpec as P

DP = ("dp_0", "dp_1")
DP_HYPER = ("dp_0", "dp_1", "hyper")
HYPER_DP = ("hyper", "dp_0", "dp_1")


def sent_to_all(value, axis):
    copies = jnp.broadcast_to(value, (lax.axis_size(axis), *value.shape))
    return lax.all_to_all(copies, axis, split_axis=0, concat_axis=0, tiled=True)


def laid_out(tiles, dim):
    lengths = list(tiles.shape[1:])
    lengths[dim] *= tiles.shape[0]
    return jnp.moveaxis(tiles, 0, dim).reshape(lengths)


def gather_directly(value, axis, dim):
    tiles = sent_to_all(value, axis)
    return laid_out(tiles, dim)


def own_rows(terms, axes):
    total = terms.astype(jnp.bfloat16)
    for axis in axes:
        total = lax.psum_scatter(total, axis, scatter_dimension=0, tiled=True)
    return total.astype(jnp.float32)


def silu_slope(values):
    logistic = jax.nn.sigmoid(values)
    return logistic * (1.0 + values * (1.0 - logistic))


def class_grads(logits, slot_labels, row_count):
    largest = jnp.max(logits, axis=-1, keepdims=True)
    exponent = jnp.exp(logits - largest)
    probability = exponent / jnp.sum(exponent, axis=-1, keepdims=True)
    classes = jnp.arange(logits.shape[-1], dtype=jnp.int32)
    onehot = (slot_labels[..., None] == classes).astype(jnp.float32)
    return ((probability - onehot) / row_count).astype(jnp.bfloat16)


def local(
    inputs, labels, client_ids, ext_weight, ext_bias, embeddings, hyper_in, hyper_bias, hyper_out
):
    slot_count, row_count, width_in = inputs.shape
    width = ext_weight.shape[1]
    flat_in = inputs.reshape(slot_count * row_count, width_in)
    preact = jnp.dot(flat_in, ext_weight, preferred_element_type=jnp.float32) + ext_bias.astype(
        jnp.float32
    )
    features = jax.nn.silu(preact).astype(jnp.bfloat16).reshape(slot_count, row_count, width)
    row_ids = gather_directly(client_ids, "hyper", 0)
    table_ids = jnp.arange(embeddings.shape[0], dtype=jnp.int32)
    select = (row_ids[:, None] == table_ids[None, :]).astype(jnp.bfloat16)
    picked = jnp.dot(select, embeddings, preferred_element_type=jnp.float32).astype(jnp.bfloat16)
    hyper_preact = jnp.dot(picked, hyper_in, preferred_element_type=jnp.float32) + hyper_bias
    hidden = jax.nn.silu(hyper_preact).astype(jnp.bfloat16)
    head_part = jnp.einsum(
        "kh,dhc->kdc", hidden, hyper_out, preferred_element_type=jnp.float32
    ).astype(jnp.bfloat16)
    feat_cols = lax.all_to_all(features, "hyper", split_axis=2, concat_axis=0, tiled=True)
    logits = lax.psum_scatter(
        jnp.einsum("krd,kdc->krc", feat_cols, head_part, preferred_element_type=jnp.float32),
        "hyper",
        scatter_dimension=0,
        tiled=True,
    )
    dlogits = class_grads(logits, labels, row_count)
    dlog_rows = lax.all_gather(dlogits, "hyper", axis=0, tiled=True)
    dhead_part = jnp.einsum(
        "krd,krc->kdc", feat_cols, dlog_rows, preferred_element_type=jnp.float32
    ).astype(jnp.bfloat16)
    dfeat_cols = jnp.einsum(
        "krc,kdc->krd", dlog_rows, head_part, preferred_element_type=jnp.float32
    ).astype(jnp.bfloat16)
    dfeatures = lax.all_to_all(dfeat_cols, "hyper", split_axis=0, concat_axis=2, tiled=True)
    dpreact = (
        dfeatures.reshape(slot_count * row_count, width).astype(jnp.float32) * silu_slope(preact)
    ).astype(jnp.bfloat16)
    grad_weight = jnp.dot(flat_in.T, dpreact, preferred_element_type=jnp.float32)
    grad_bias = jnp.sum(dpreact.astype(jnp.float32), axis=0)
    grad_out = own_rows(
        jnp.einsum("kh,kdc->dhc", hidden, dhead_part, preferred_element_type=jnp.float32), DP
    )
    dhidden = jnp.einsum("kdc,dhc->kh", dhead_part, hyper_out, preferred_element_type=jnp.float32)
    hyper_dpre = dhidden * silu_slope(hyper_preact)
    grad_in = jnp.dot(picked.astype(jnp.float32).T, hyper_dpre)
    grad_hbias = jnp.sum(hyper_dpre, axis=0)
    back_rows = jnp.dot(hyper_dpre, hyper_in.astype(jnp.float32).T)
    grad_table = jnp.dot(select.astype(jnp.float32).T, back_rows)
    grad_weight, grad_bias, grad_table, grad_in, grad_hbias = lax.psum(
        (grad_weight, grad_bias, grad_table, grad_in, grad_hbias), DP_HYPER
    )
    return (grad_weight, grad_bias, grad_table, grad_in, grad_hbias, grad_out)


def solution(mesh):
    torus = Mesh(mesh.devices.reshape(4, 4, mesh.shape["hyper"]), ("dp_0", "dp_1", "hyper"))
    placed = (
        P(DP_HYPER, None, None),
        P(DP_HYPER, None),
        P(DP_HYPER),
        P(),
        P(),
        P(),
        P(),
        P(),
        P("hyper", None, None),
    )
    return jax.shard_map(
        local,
        mesh=torus,
        in_specs=placed,
        out_specs=(P(), P(), P(), P(), P(), P(HYPER_DP, None, None)),
        check_vma=False,
    )
```

profile of v0, /device:TPU:1, one launch (start us, length us, event | category | flops | bytes accessed | tf_op | source)
XLA Modules:
  0.0 629.8 jit_solution(14461696702569586145)
XLA Ops:
  8.5 12.6 %all-to-all-start.1 = ((s32[16,1,2]{2,1,0:T(1,128)}), s32[16,1,2]{2,1,0:T(1,128)S(1)}, u32[]{:S(2)}, u32[]{:S(2)}) async-start(s32[16,1,2]{2,1,0:T(1,128)} %broadcast_in_dim.2), calls=%async_computation.1 | async-start | bytes 16384 | tf_op jit(solution)/shard_map/all_to_all | solution.py:14
  21.8 3.1 multiply_convert_fusion.1
  24.9 5.0 copy.35
  30.0 2.2 reshape.50
  32.3 9.6 %all-to-all-start = ((bf16[16,2,16384]{2,1,0:T(2,128)(2,1)}), bf16[16,2,16384]{2,1,0:T(2,128)(2,1)S(1)}, u32[]{:S(2)}, u32[]{:S(2)}) async-start(bf16[16,2,16384]{2,1,0:T(2,128)(2,1)} %reshape.50), calls=%async_computation | async-start | bytes 2097152 | tf_op jit(solution)/shard_map/all_to_all | solution.py:68
  43.6 10.5 %fusion.9 = bf16[32,256,256]{2,0,1:T(8,128)(2,1)} fusion(bf16[256,50,256]{2,0,1:T(8,128)(2,1)} %param.17, f32[32,50]{1,0:T(8,128)S(1)} %convolution_add_fusion.1), kind=kOutput, calls=%fused_computation.12 | convolution fusion | flops 211820352 | bytes 10754304 | tf_op jit(solution)/shard_map/kh,dhc->kdc/dot_general | solution.py:65
  54.1 9.6 %all-to-all-done = bf16[16,2,16384]{2,1,0:T(2,128)(2,1)S(1)} async-done(((bf16[16,2,16384]{2,1,0:T(2,128)(2,1)}), bf16[16,2,16384]{2,1,0:T(2,128)(2,1)S(1)}, u32[]{:S(2)}, u32[]{:S(2)}) %all-to-all-start) | async-done | bytes 1048608 | tf_op jit(solution)/shard_map/all_to_all | solution.py:68
  63.7 2.4 reshape.51
  66.1 4.5 copy.36
  70.6 6.0 fusion.7
  76.6 89.9 %reduce-scatter.4.cloned.1.call-done = f32[2,64,256]{2,1,0:T(8,128)} async-done(((f32[32,64,256]{2,1,0:T(8,128)}), f32[2,64,256]{2,1,0:T(8,128)}) %reduce-scatter.4.cloned.1.call-update) | async-done | bytes 131088 | tf_op jit(solution)/shard_map/reduce_scatter | solution.py:69
  168.7 55.2 %all-gather.2.cloned.1.call-done = bf16[32,64,256]{2,1,0:T(8,128)(2,1)} async-done(((bf16[2,64,256]{2,1,0:T(8,128)(2,1)}), bf16[32,64,256]{2,1,0:T(8,128)(2,1)}) %all-gather.2.cloned.1.call-update) | async-done | bytes 1048592 | tf_op jit(solution)/shard_map/all_gather | solution.py:76
  223.8 2.5 convolution_convert_fusion
  228.3 6.0 convert_bitcast_fusion
  235.6 5.7 fusion.12
  241.3 4.0 all-to-all-start.2
  245.6 11.3 %copy.42 = bf16[256,50,256]{0,1,2:T(8,128)(2,1)} copy(bf16[256,50,256]{2,0,1:T(8,128)(2,1)} %param.17) | data formatting | bytes 13107200 | tf_op args[8]
  256.9 8.0 %copy.41 = bf16[32,256,256]{1,0,2:T(8,128)(2,1)} copy(bf16[32,256,256]{2,1,0:T(8,128)(2,1)} %copy-done.1) | data formatting | bytes 8388608 | tf_op jit(solution)/shard_map/convert_element_type | solution.py:79
  264.9 6.5 %fusion.30 = (f32[50]{0:T(128)S(1)}, bf16[32,50]{1,0:T(8,128)(2,1)S(1)}) fusion(f32[32,50]{1,0:T(8,128)S(1)} %convolution_add_fusion.1, bf16[32,256,256]{1,0,2:T(8,128)(2,1)} %copy.41, bf16[256,50,256]{0,1,2:T(8,128)(2,1)} %copy.42), kind=kOutput, calls=%fused_computation.40 | convolution fusion | flops 209731152 | bytes 10757704 | tf_op jit(solution)/shard_map/kdc,dhc->kh/dot_general | solution.py:92
  277.5 27.3 %reduce-scatter.6.cloned.1.call-done = bf16[64,50,256]{2,1,0:T(8,128)(2,1)} async-done(((bf16[256,50,256]{2,1,0:T(8,128)(2,1)}), bf16[64,50,256]{2,1,0:T(8,128)(2,1)}) %reduce-scatter.6.cloned.1.call-update) | async-done | bytes 1638416 | tf_op jit(solution)/shard_map/reduce_scatter | solution.py:31
  305.0 76.7 %all-reduce = (f32[4096]{0:T(1024)}, f32[128,50]{0,1:T(8,128)}, f32[50]{0:T(128)}) all-reduce(f32[4096]{0:T(1024)S(1)} %get-tuple-element.29, f32[128,50]{0,1:T(8,128)S(1)} %fusion.31, f32[50]{0:T(128)S(1)} %get-tuple-element.33), channel_id=1, replica_groups=mesh['dp_0'=4,'dp_1'=4,'hyper'=16] {'dp_0','dp_1','hyper'}, use_global_device_ids=true, to_apply=%region_5.6 | all-reduce | flops 10546 | bytes 84368 | tf_op jit(solution)/shard_map/psum | solution.py:98
  381.7 191.7 %all-reduce.4.cloned.1.call-done = (f32[128,4096]{0,1:T(8,128)}, f32[512,128]{1,0:T(8,128)}) async-done(((f32[128,4096]{0,1:T(8,128)}, f32[512,128]{1,0:T(8,128)}), (f32[128,4096]{0,1:T(8,128)}, f32[512,128]{1,0:T(8,128)})) %all-reduce.4.cloned.1.call-update) | async-done | bytes 2359312 | tf_op jit(solution)/shard_map/psum | solution.py:98
  573.3 2.9 copy.44
  576.3 44.3 %reduce-scatter.8.cloned.1.call-done = bf16[16,50,256]{2,1,0:T(8,128)(2,1)} async-done(((bf16[64,50,256]{2,1,0:T(8,128)(2,1)}), bf16[16,50,256]{2,1,0:T(8,128)(2,1)}) %reduce-scatter.8.cloned.1.call-update) | async-done | bytes 409616 | tf_op jit(solution)/shard_map/reduce_scatter | solution.py:31
  (48 shorter events, 18.2 us)
Async XLA Ops:
  7.2 14.7 %copy-start = (bf16[128,4096]{1,0:T(8,128)(2,1)S(1)}, bf16[128,4096]{1,0:T(8,128)(2,1)}, u32[]{:S(2)}) copy-start(bf16[128,4096]{1,0:T(8,128)(2,1)} %param.12) | copy-start | bytes 3145732
  8.5 23.7 %all-to-all-start.1 = ((s32[16,1,2]{2,1,0:T(1,128)}), s32[16,1,2]{2,1,0:T(1,128)S(1)}, u32[]{:S(2)}, u32[]{:S(2)}) async-start(s32[16,1,2]{2,1,0:T(1,128)} %broadcast_in_dim.2), calls=%async_computation.1 | async-start | bytes 16384 | tf_op jit(solution)/shard_map/all_to_all | solution.py:14
  30.0 13.2 %copy-start.8 = (bf16[512,128]{1,0:T(8,128)(2,1)S(1)}, bf16[512,128]{1,0:T(8,128)(2,1)}, u32[]{:S(2)}) copy-start(bf16[512,128]{1,0:T(8,128)(2,1)} %param.14) | copy-start | bytes 393220
  30.0 13.4 %copy-start.5 = (bf16[128,50]{0,1:T(8,128)(2,1)S(1)}, bf16[128,50]{0,1:T(8,128)(2,1)}, u32[]{:S(2)}) copy-start(bf16[128,50]{0,1:T(8,128)(2,1)} %param.15) | copy-start | bytes 38404
  30.0 13.4 %copy-start.7 = (f32[50]{0:T(128)S(1)}, f32[50]{0:T(128)}, u32[]{:S(2)}) copy-start(f32[50]{0:T(128)} %param.16) | copy-start | bytes 604
  32.3 31.4 %all-to-all-start = ((bf16[16,2,16384]{2,1,0:T(2,128)(2,1)}), bf16[16,2,16384]{2,1,0:T(2,128)(2,1)S(1)}, u32[]{:S(2)}, u32[]{:S(2)}) async-start(bf16[16,2,16384]{2,1,0:T(2,128)(2,1)} %reshape.50), calls=%async_computation | async-start | bytes 2097152 | tf_op jit(solution)/shard_map/all_to_all | solution.py:68
  41.9 124.6 %reduce-scatter.4.cloned.1.call-start = ((), (), s32[]{:S(2)}) async-start(), calls=%async_computation.6 | async-start | bytes 2228224 | tf_op jit(solution)/shard_map/reduce_scatter | solution.py:69
  76.5 90.0 %copy-start.9 = (s32[2,64]{1,0:T(2,128)S(1)}, s32[2,64]{1,0:T(2,128)}, u32[]{:S(2)}) copy-start(s32[2,64]{1,0:T(2,128)} %param.10) | copy-start | bytes 1540
  76.6 147.3 %all-gather.2.cloned.1.call-start = ((), (), s32[]{:S(2)}) async-start(), calls=%async_computation.7 | async-start | bytes 1114112 | tf_op jit(solution)/shard_map/all_gather | solution.py:76
  168.4 136.4 %reduce-scatter.6.cloned.1.call-start = ((), (), s32[]{:S(2)}) async-start(), calls=%async_computation.8 | async-start | bytes 9175040 | tf_op jit(solution)/shard_map/reduce_scatter | solution.py:31
  226.4 2.0 copy-start.1
  234.4 1.2 copy-start.2
  241.3 31.1 %all-to-all-start.2 = ((bf16[32,64,256]{2,1,0:T(8,128)(2,1)}), bf16[32,64,256]{2,1,0:T(8,128)(2,1)S(1)}, u32[]{:S(2)}, u32[]{:S(2)}) async-start(bf16[32,64,256]{2,1,0:T(8,128)(2,1)} %fusion.12), calls=%async_computation.3 | async-start | bytes 2097152 | tf_op jit(solution)/shard_map/all_to_all | solution.py:83
  245.3 328.0 %all-reduce.4.cloned.1.call-start = ((), (), s32[]{:S(2)}) async-start(), calls=%async_computation.10 | async-start | bytes 4718592 | tf_op jit(solution)/shard_map/psum | solution.py:98
  273.0 1.7 copy-start.3
  274.7 0.8 copy-start.6
  277.4 343.2 %reduce-scatter.8.cloned.1.call-start = ((), (), s32[]{:S(2)}) async-start(), calls=%async_computation.9 | async-start | bytes 2293760 | tf_op jit(solution)/shard_map/reduce_scatter | solution.py:31
  573.3 49.3 %copy-start.4 = (f32[512,128]{1,0:T(8,128)S(1)}, f32[512,128]{1,0:T(8,128)}, u32[]{:S(2)}) copy-start(f32[512,128]{1,0:T(8,128)} %get-tuple-element.39) | copy-start | bytes 786436
Sparse Core Ops, SparseCore 0:
  76.7 89.7 reduce-scatter.3
  169.8 54.0 all-gather.1
  234.5 70.2 reduce-scatter.5
  310.7 262.5 all-reduce.3
  575.7 44.7 reduce-scatter.7
where the time goes:
time: 631 us; the launch traced here: 630 us
  waiting for transfers between devices  418 us (66%)
  blocking collectives  76.7 us (12%)
  local copies, waits for them, and re-layouts  46.5 us (7%)
  matrix products  43.7 us (7%)
  starting transfers between devices  26.8 us (4%)
  between operations  13.9 us (2%)
    psum x1, waiting for transfers between devices, local(): lax.psum((grad_weight, grad_bias, grad_table, grad_in, grad_hbias), DP_HY...  192 us
    reduce_scatter x1, waiting for transfers between devices, local(): lax.psum_scatter(jnp.einsum('krd,kdc->krc', feat_cols, head_part, preferr...  89.9 us
    psum x1, blocking collectives, local(): lax.psum((grad_weight, grad_bias, grad_table, grad_in, grad_hbias), DP_HY...  76.7 us
    reduce_scatter x2, waiting for transfers between devices, own_rows(): total = lax.psum_scatter(total, axis, scatter_dimension=0, tiled=True)  71.6 us
    all_gather x1, waiting for transfers between devices, local(): dlog_rows = lax.all_gather(dlogits, 'hyper', axis=0, tiled=True)  55.2 us
    unnamed x27, local copies, waits for them, and re-layouts  26.5 us
  transfers between devices with their start and end apart: 8, of which 6 were waited for; matrix products, arithmetic and copies ran while one was open for 10% of the time, Pallas kernels for 0%

commit v1 on v0

--- a/solution.py
+++ b/solution.py
@@ -3,6 +3,7 @@
 from jax import lax
 from jax.sharding import Mesh
 from jax.sharding import PartitionSpec as P
+from jax.lax import all_to_all, axis_size
 
 DP = ("dp_0", "dp_1")
 DP_HYPER = ("dp_0", "dp_1", "hyper")
@@ -73,7 +74,16 @@
         tiled=True,
     )
     dlogits = class_grads(logits, labels, row_count)
-    dlog_rows = lax.all_gather(dlogits, "hyper", axis=0, tiled=True)
+
+    def write_the_rails(field):
+        sides = []
+        for _ in range(axis_size("hyper")):
+            sides.append(field)
+        y_new = jnp.stack(sides)
+        block_next = all_to_all(y_new, "hyper", split_axis=0, concat_axis=0)
+        return jnp.concatenate(block_next, 0)
+
+    dlog_rows = write_the_rails(dlogits)
     dhead_part = jnp.einsum(
         "krd,krc->kdc", feat_cols, dlog_rows, preferred_element_type=jnp.float32
     ).astype(jnp.bfloat16)

time: 631 us -> 607 us (0.962)
  waiting for transfers between devices: 418 us -> 375 us
  blocking collectives: 76.7 us -> 103 us
    all_gather x1 -> x0, waiting for transfers between devices: 55.2 us -> none  [local(): dlog_rows = lax.all_gather(dlogits, 'hyper', axis=0, tiled=True)]
    all_to_all x0 -> x1, blocking collectives: none -> 25.9 us  [write_the_rails(): block_next = all_to_all(y_new, 'hyper', split_axis=0, concat_axis=0)]
    reduce_scatter x2, waiting for transfers between devices: 71.6 us -> 83.5 us  [own_rows(): total = lax.psum_scatter(total, axis, scatter_dimension=0, tiled=True)]
  transfers between devices with their start and end apart: 8 -> 7, of which waited for: 6 -> 5; matrix products, arithmetic and copies ran while one was open for 10% -> 11% of each run, Pallas kernels for 0% -> 0%
where the time goes in v1:
time: 607 us; the launch traced here: 606 us
  waiting for transfers between devices  375 us (62%)
  blocking collectives  103 us (17%)
  matrix products  42.5 us (7%)
  local copies, waits for them, and re-layouts  41.4 us (7%)
  starting transfers between devices  27.2 us (4%)
  between operations  13.9 us (2%)
    psum x1, waiting for transfers between devices, local(): lax.psum((grad_weight, grad_bias, grad_table, grad_in, grad_hbias), DP_HY...  192 us
    reduce_scatter x1, waiting for transfers between devices, local(): lax.psum_scatter(jnp.einsum('krd,kdc->krc', feat_cols, head_part, preferr...  89.9 us
    reduce_scatter x2, waiting for transfers between devices, own_rows(): total = lax.psum_scatter(total, axis, scatter_dimension=0, tiled=True)  83.5 us
    psum x1, blocking collectives, local(): lax.psum((grad_weight, grad_bias, grad_table, grad_in, grad_hbias), DP_HY...  76.7 us
    all_to_all x1, blocking collectives, write_the_rails(): block_next = all_to_all(y_new, 'hyper', split_axis=0, concat_axis=0)  25.9 us
    unnamed x27, local copies, waits for them, and re-layouts  24.5 us
    all_to_all x1, starting transfers between devices, sent_to_all(): return lax.all_to_all(copies, axis, split_axis=0, concat_axis=0, tiled=True)  12.6 us
  transfers between devices with their start and end apart: 7, of which 5 were waited for; matrix products, arithmetic and copies ran while one was open for 11% of the time, Pallas kernels for 0%

profile of v1, /device:TPU:1, one launch (start us, length us, event | category | flops | bytes accessed | tf_op | source)
XLA Modules:
  0.0 606.0 jit_solution(4629020946109746182)
XLA Ops:
  8.5 12.6 %all-to-all-start.1 = ((s32[16,1,2]{2,1,0:T(1,128)}), s32[16,1,2]{2,1,0:T(1,128)S(1)}, u32[]{:S(2)}, u32[]{:S(2)}) async-start(s32[16,1,2]{2,1,0:T(1,128)} %broadcast_in_dim.2), calls=%async_computation.1 | async-start | bytes 16384 | tf_op jit(solution)/shard_map/all_to_all | solution.py:15
  21.8 3.1 multiply_convert_fusion.1
  24.9 5.0 copy.35
  30.0 2.2 reshape.56
  32.3 9.6 %all-to-all-start = ((bf16[16,2,16384]{2,1,0:T(2,128)(2,1)}), bf16[16,2,16384]{2,1,0:T(2,128)(2,1)S(1)}, u32[]{:S(2)}, u32[]{:S(2)}) async-start(bf16[16,2,16384]{2,1,0:T(2,128)(2,1)} %reshape.56), calls=%async_computation | async-start | bytes 2097152 | tf_op jit(solution)/shard_map/all_to_all | solution.py:69
  43.6 10.5 %fusion.9 = bf16[32,256,256]{2,0,1:T(8,128)(2,1)} fusion(bf16[256,50,256]{2,0,1:T(8,128)(2,1)} %param.17, f32[32,50]{1,0:T(8,128)S(1)} %convolution_add_fusion.1), kind=kOutput, calls=%fused_computation.12 | convolution fusion | flops 211820352 | bytes 10754304 | tf_op jit(solution)/shard_map/kh,dhc->kdc/dot_general | solution.py:66
  54.1 9.7 %all-to-all-done = bf16[16,2,16384]{2,1,0:T(2,128)(2,1)S(1)} async-done(((bf16[16,2,16384]{2,1,0:T(2,128)(2,1)}), bf16[16,2,16384]{2,1,0:T(2,128)(2,1)S(1)}, u32[]{:S(2)}, u32[]{:S(2)}) %all-to-all-start) | async-done | bytes 1048608 | tf_op jit(solution)/shard_map/all_to_all | solution.py:69
  66.3 5.9 fusion.7
  72.3 89.9 %reduce-scatter.4.cloned.1.call-done = f32[2,64,256]{2,1,0:T(8,128)} async-done(((f32[32,64,256]{2,1,0:T(8,128)}), f32[2,64,256]{2,1,0:T(8,128)}) %reduce-scatter.4.cloned.1.call-update) | async-done | bytes 131088 | tf_op jit(solution)/shard_map/reduce_scatter | solution.py:70
  163.5 25.9 %all_to_all.38 = bf16[16,2,64,256]{3,2,1,0:T(8,128)(2,1)S(1)} all-to-all(bf16[16,2,64,256]{3,2,1,0:T(8,128)(2,1)S(1)} %stack.2), channel_id=1, replica_groups=mesh['dp_0'=4,'dp_1'=4,'hyper'=16] {'hyper'}, dimensions={0} | all-to-all | bytes 2097152 | tf_op jit(solution)/shard_map/all_to_all | solution.py:83
  190.8 1.9 copy-done.2
  192.7 6.0 convert_bitcast_fusion
  198.8 5.7 fusion.12
  204.5 4.6 all-to-all-start.3
  209.4 11.6 %copy.42 = bf16[256,50,256]{0,1,2:T(8,128)(2,1)} copy(bf16[256,50,256]{2,0,1:T(8,128)(2,1)} %param.17) | data formatting | bytes 13107200 | tf_op args[8]
  221.0 7.9 %copy.41 = bf16[32,256,256]{1,0,2:T(8,128)(2,1)} copy(bf16[32,256,256]{2,1,0:T(8,128)(2,1)} %copy-done.2) | data formatting | bytes 8388608 | tf_op jit(solution)/shard_map/convert_element_type | solution.py:89
  228.9 6.5 %fusion.30 = (f32[50]{0:T(128)S(1)}, bf16[32,50]{1,0:T(8,128)(2,1)S(1)}) fusion(f32[32,50]{1,0:T(8,128)S(1)} %convolution_add_fusion.1, bf16[32,256,256]{1,0,2:T(8,128)(2,1)} %copy.41, bf16[256,50,256]{0,1,2:T(8,128)(2,1)} %copy.42), kind=kOutput, calls=%fused_computation.40 | convolution fusion | flops 209731152 | bytes 10757704 | tf_op jit(solution)/shard_map/kdc,dhc->kh/dot_general | solution.py:102
  239.7 1.8 convolution_bitcast_fusion
  241.5 39.3 %reduce-scatter.6.cloned.1.call-done = bf16[64,50,256]{2,1,0:T(8,128)(2,1)} async-done(((bf16[256,50,256]{2,1,0:T(8,128)(2,1)}), bf16[64,50,256]{2,1,0:T(8,128)(2,1)}) %reduce-scatter.6.cloned.1.call-update) | async-done | bytes 1638416 | tf_op jit(solution)/shard_map/reduce_scatter | solution.py:32
  281.0 76.7 %all-reduce = (f32[4096]{0:T(1024)}, f32[128,50]{0,1:T(8,128)}, f32[50]{0:T(128)}) all-reduce(f32[4096]{0:T(1024)S(1)} %get-tuple-element.29, f32[128,50]{0,1:T(8,128)S(1)} %fusion.31, f32[50]{0:T(128)S(1)} %get-tuple-element.33), channel_id=1, replica_groups=mesh['dp_0'=4,'dp_1'=4,'hyper'=16] {'dp_0','dp_1','hyper'}, use_global_device_ids=true, to_apply=%region_5.6 | all-reduce | flops 10546 | bytes 84368 | tf_op jit(solution)/shard_map/psum | solution.py:108
  357.7 191.8 %all-reduce.4.cloned.1.call-done = (f32[128,4096]{0,1:T(8,128)}, f32[512,128]{1,0:T(8,128)}) async-done(((f32[128,4096]{0,1:T(8,128)}, f32[512,128]{1,0:T(8,128)}), (f32[128,4096]{0,1:T(8,128)}, f32[512,128]{1,0:T(8,128)})) %all-reduce.4.cloned.1.call-update) | async-done | bytes 2359312 | tf_op jit(solution)/shard_map/psum | solution.py:108
  549.5 3.0 copy.44
  552.5 44.3 %reduce-scatter.8.cloned.1.call-done = bf16[16,50,256]{2,1,0:T(8,128)(2,1)} async-done(((bf16[64,50,256]{2,1,0:T(8,128)(2,1)}), bf16[16,50,256]{2,1,0:T(8,128)(2,1)}) %reduce-scatter.8.cloned.1.call-update) | async-done | bytes 409616 | tf_op jit(solution)/shard_map/reduce_scatter | solution.py:32
  596.7 2.0 copy.45
  (47 shorter events, 14.4 us)
Async XLA Ops:
  7.2 14.7 %copy-start = (bf16[128,4096]{1,0:T(8,128)(2,1)S(1)}, bf16[128,4096]{1,0:T(8,128)(2,1)}, u32[]{:S(2)}) copy-start(bf16[128,4096]{1,0:T(8,128)(2,1)} %param.12) | copy-start | bytes 3145732
  8.5 23.7 %all-to-all-start.1 = ((s32[16,1,2]{2,1,0:T(1,128)}), s32[16,1,2]{2,1,0:T(1,128)S(1)}, u32[]{:S(2)}, u32[]{:S(2)}) async-start(s32[16,1,2]{2,1,0:T(1,128)} %broadcast_in_dim.2), calls=%async_computation.1 | async-start | bytes 16384 | tf_op jit(solution)/shard_map/all_to_all | solution.py:15
  30.0 13.2 %copy-start.8 = (bf16[512,128]{1,0:T(8,128)(2,1)S(1)}, bf16[512,128]{1,0:T(8,128)(2,1)}, u32[]{:S(2)}) copy-start(bf16[512,128]{1,0:T(8,128)(2,1)} %param.14) | copy-start | bytes 393220
  30.0 13.4 %copy-start.5 = (bf16[128,50]{0,1:T(8,128)(2,1)S(1)}, bf16[128,50]{0,1:T(8,128)(2,1)}, u32[]{:S(2)}) copy-start(bf16[128,50]{0,1:T(8,128)(2,1)} %param.15) | copy-start | bytes 38404
  30.0 13.4 %copy-start.7 = (f32[50]{0:T(128)S(1)}, f32[50]{0:T(128)}, u32[]{:S(2)}) copy-start(f32[50]{0:T(128)} %param.16) | copy-start | bytes 604
  32.3 31.5 %all-to-all-start = ((bf16[16,2,16384]{2,1,0:T(2,128)(2,1)}), bf16[16,2,16384]{2,1,0:T(2,128)(2,1)S(1)}, u32[]{:S(2)}, u32[]{:S(2)}) async-start(bf16[16,2,16384]{2,1,0:T(2,128)(2,1)} %reshape.56), calls=%async_computation | async-start | bytes 2097152 | tf_op jit(solution)/shard_map/all_to_all | solution.py:69
  41.9 120.3 %reduce-scatter.4.cloned.1.call-start = ((), (), s32[]{:S(2)}) async-start(), calls=%async_computation.7 | async-start | bytes 2228224 | tf_op jit(solution)/shard_map/reduce_scatter | solution.py:70
  72.2 89.9 %copy-start.9 = (s32[2,64]{1,0:T(2,128)S(1)}, s32[2,64]{1,0:T(2,128)}, u32[]{:S(2)}) copy-start(s32[2,64]{1,0:T(2,128)} %param.10) | copy-start | bytes 1540
  72.3 208.5 %reduce-scatter.6.cloned.1.call-start = ((), (), s32[]{:S(2)}) async-start(), calls=%async_computation.8 | async-start | bytes 9175040 | tf_op jit(solution)/shard_map/reduce_scatter | solution.py:32
  190.8 2.0 copy-start.2
  204.5 32.0 %all-to-all-start.3 = ((bf16[32,64,256]{2,1,0:T(8,128)(2,1)}), bf16[32,64,256]{2,1,0:T(8,128)(2,1)S(1)}, u32[]{:S(2)}, u32[]{:S(2)}) async-start(bf16[32,64,256]{2,1,0:T(8,128)(2,1)} %fusion.12), calls=%async_computation.4 | async-start | bytes 2097152 | tf_op jit(solution)/shard_map/all_to_all | solution.py:93
  209.1 340.4 %all-reduce.4.cloned.1.call-start = ((), (), s32[]{:S(2)}) async-start(), calls=%async_computation.10 | async-start | bytes 4718592 | tf_op jit(solution)/shard_map/psum | solution.py:108
  237.1 1.7 copy-start.3
  238.8 0.8 copy-start.6
  241.5 355.2 %reduce-scatter.8.cloned.1.call-start = ((), (), s32[]{:S(2)}) async-start(), calls=%async_computation.9 | async-start | bytes 2293760 | tf_op jit(solution)/shard_map/reduce_scatter | solution.py:32
  549.5 50.0 %copy-start.1 = (bf16[128,4096]{1,0:T(8,128)(2,1)S(1)}, bf16[128,4096]{1,0:T(8,128)(2,1)}, u32[]{:S(2)}) copy-start(bf16[128,4096]{1,0:T(8,128)(2,1)} %param.12) | copy-start | bytes 3145732
  549.5 49.3 %copy-start.4 = (f32[512,128]{1,0:T(8,128)S(1)}, f32[512,128]{1,0:T(8,128)}, u32[]{:S(2)}) copy-start(f32[512,128]{1,0:T(8,128)} %get-tuple-element.39) | copy-start | bytes 786436
Sparse Core Ops, SparseCore 0:
  72.4 89.7 reduce-scatter.3
  198.9 81.8 reduce-scatter.5
  286.9 262.5 all-reduce.3
  551.9 44.7 reduce-scatter.7
